TPU v7x, 32 devices: a whole 2x2x4 slice. The times are simulated.
32 devices in a mesh: pair: 4 (over z), aux: 8 (over y, x, core).
Axes of the slice: x: 2, y: 2, z: 4, core: 2. Of those that a mesh axis runs over, the one named last changes fastest.
Arguments:
- integrals: bfloat16 [12288, 12288], P('pair', 'aux'), may hold values from -0.1875 to 0.1875
- energy_gaps: float32 [12288], P('pair'), may hold values from 0.3 to 3
- trial_vectors: float32 [12288, 64], P('pair'), may hold values from -160 to 160
Outputs:
- sigma_vectors: float32 [12288, 64], P(('pair', 'aux'))
- subspace: float32 [64, 64], replicated
- residuals: float32 [12288, 64], P(('pair', 'aux'))
- residual_norms: float32 [64], replicated
All inputs are finite; a program needn't handle non-finite values.
Results may differ from a plain program's by a relative error of at most 0.0052.
Values may be sent and summed in bfloat16 or wider, within the bound.
A program may use at most 64 MiB of HBM per device.

v0:
```python
import functools

import jax
import jax.numpy as jnp
from jax import lax
from jax.experimental import pallas as pl
from jax.experimental.pallas import tpu as pltpu
from jax.sharding import PartitionSpec as P

epsilon = 1e-06
MESH = pl.DeviceIdType.MESH
f32, bf16 = jnp.float32, jnp.bfloat16
WIDTH = 256
VMEM = 67043328
LAG = 3
NT = (((1,), (1,)), ((), ()))


def exact(a, b):
    return lax.dot_general(a, b, NT, precision=lax.Precision.HIGHEST, preferred_element_type=f32)


def kernel(
    np_, na, chunks, width, share,
    ints_hbm, gaps_hbm, trial_hbm,
    sigma_hbm, sub_hbm, res_hbm, norm_hbm,
    ints, gaps, trial, half, own, acc, mat, gram,
    pre_in, pre_out, suf_in, suf_out,
    b1_out, b1_in, b2_out, b2_in,
    m1_out, m1_in, m2, m3, n1, n2,
    sigma, sub, res, norm,
    load, aload, pre_s, pre_r, suf_s, suf_r,
    b1_s, b1_r, b2_s, b2_r, m1_s, m1_r, m2_s, m2_r, m3_s, m3_r, n1_s, n1_r, n2_s, n2_r, store,
):
    z, a = lax.axis_index("pair"), lax.axis_index("aux")
    core, chip, chips = a % 2, a // 2, na // 2
    vecs = trial.shape[0]

    trial_load = pltpu.make_async_copy(trial_hbm, trial, aload.at[0])
    gaps_load = pltpu.make_async_copy(gaps_hbm, gaps, aload.at[1])
    trial_load.start()
    loads = [
        pltpu.make_async_copy(ints_hbm.at[:, pl.ds(c * width, width)], ints.at[c], load.at[c])
        for c in range(chunks)
    ]
    loads[0].start()
    gaps_load.start()
    for c in range(1, chunks):
        loads[c].start()

    barrier = pltpu.get_barrier_semaphore()
    for d in range(1, np_):
        pl.semaphore_signal(barrier, inc=1, device_id={"pair": (z + d) % np_, "aux": a}, device_id_type=MESH)
    for d in range(1, na):
        pl.semaphore_signal(barrier, inc=1, device_id={"pair": z, "aux": (a + d) % na}, device_id_type=MESH)

    def remote(src, dst, s, r, pair, aux):
        return pltpu.make_async_remote_copy(
            src_ref=src, dst_ref=dst, send_sem=s, recv_sem=r,
            device_id={"pair": pair, "aux": aux}, device_id_type=MESH,
        )

    def prefix(c):
        return remote(pre_out.at[c], pre_in.at[c], pre_s.at[c], pre_r.at[c], z + 1, a)

    def suffix(c):
        return remote(suf_out.at[c], suf_in.at[c], suf_s.at[c], suf_r.at[c], z - 1, a)

    acc[...] = jnp.zeros_like(acc)
    mat[...] = jnp.zeros_like(mat)
    trial_load.wait()
    half[...] = trial[...].astype(bf16)
    gaps_load.wait()
    first = pl.multiple_of(a * share, 128)
    rows = share // 128

    def own_trial():
        return trial[:, pl.ds(first, share)]

    def own_gaps():
        return jnp.concatenate([gaps[pl.ds(a * rows + q, 1), :] for q in range(rows)], axis=1)

    eye = lax.broadcasted_iota(jnp.int32, (vecs, vecs), 0) == lax.broadcasted_iota(jnp.int32, (vecs, vecs), 1)

    def as_row(column):
        return jnp.sum(jnp.where(eye, column, 0.0), axis=0, keepdims=True)

    mine = own_trial()
    gram[...] = exact(mine, mine * own_gaps())
    pl.semaphore_wait(barrier, np_ - 1 + na - 1)

    after = np_ - 1 - z
    longest = jnp.maximum(z, after)

    def step(t, carry):
        @pl.when(t < chunks)
        def _():
            pltpu.make_async_copy(ints_hbm.at[:, pl.ds(0, width)], ints.at[t], load.at[t]).wait()
            own[t] = jnp.dot(half[...], ints[t], preferred_element_type=f32)

        p = t - LAG * z

        @pl.when((p >= 0) & (p < chunks) & (after > 0))
        def _():
            @pl.when(z == 0)
            def _():
                pre_out[p] = own[p].astype(bf16)

            @pl.when(z > 0)
            def _():
                prefix(p).wait_recv()
                pre_out[p] = (own[p] + pre_in[p].astype(f32)).astype(bf16)

            prefix(p).start()

        s = t - LAG * after

        @pl.when((s >= 0) & (s < chunks) & (z > 0))
        def _():
            @pl.when(after == 0)
            def _():
                suf_out[s] = own[s].astype(bf16)

            @pl.when(after > 0)
            def _():
                suffix(s).wait_recv()
                suf_out[s] = (own[s] + suf_in[s].astype(f32)).astype(bf16)

            suffix(s).start()

        c = t - LAG * longest

        @pl.when((c >= 0) & (c < chunks))
        def _():
            @pl.when(z == np_ - 1)
            def _():
                prefix(c).wait_recv()

            @pl.when(z == 0)
            def _():
                suffix(c).wait_recv()

            @pl.when(z > 0)
            def _():
                own[c] = own[c] + pre_in[c].astype(f32)

            @pl.when(after > 0)
            def _():
                own[c] = own[c] + suf_in[c].astype(f32)

            aux = own[c].astype(bf16)
            for b in range(chips):
                part = lax.dot_general(
                    aux, ints[c, pl.ds(b * 2 * share, 2 * share), :], NT, preferred_element_type=f32
                )
                acc[2 * b] += part[:, :share]
                acc[2 * b + 1] += part[:, share:]

            @pl.when(c % np_ == z)
            def _():
                total = own[c]
                mat[...] += exact(total, total.astype(bf16).astype(f32))

        return carry

    lax.fori_loop(0, chunks + LAG * (np_ - 1), step, 0)

    other = chip * 2 + 1 - core
    pending = []
    product = gram[...] + 2.0 * mat[...]
    mine = own_trial()
    squares = as_row(jnp.sum(mine * mine, axis=1, keepdims=True))
    h = vecs // 2
    m1_out[0:h] = jnp.concatenate([product[:h], product[h:]], axis=1)
    m1_out[h:] = jnp.broadcast_to(jnp.concatenate([squares, squares], axis=1), (8, 2 * vecs))
    m1_copy = remote(m1_out, m1_in, m1_s, m1_r, z, other)
    m1_copy.start()
    pending.append(m1_copy)

    b1 = []
    for d in range(chips):
        j = (chip + 1 + d) % chips
        b1_out[d] = acc[2 * j + 1 - core].astype(bf16)
        copy = remote(b1_out.at[d], b1_in.at[d], b1_s.at[d], b1_r.at[d], z, other)
        copy.start()
        b1.append(copy)
        pending.append(copy)
    m1_copy.wait_recv()
    m2[chip] = m1_out[...] + m1_in[...]
    for d in range(1, chips):
        copy = remote(m2.at[chip], m2.at[chip], m2_s.at[d], m2_r.at[chip], z, ((chip + d) % chips) * 2 + core)
        copy.start()
        pending.append(copy)
    for d in range(chips - 1):
        j = (chip + 1 + d) % chips
        b1[d].wait_recv()
        b2_out[d] = (acc[2 * j + core] + b1_in[d].astype(f32)).astype(bf16)
        copy = remote(b2_out.at[d], b2_in.at[d], b2_s.at[d], b2_r.at[d], z, 2 * j + core)
        copy.start()
        pending.append(copy)
    b1[chips - 1].wait_recv()
    coupled = acc[a] + b1_in[chips - 1].astype(f32)

    for d in range(1, chips):
        j = (chip + d) % chips
        remote(m2.at[j], m2.at[j], m2_s.at[d], m2_r.at[j], z, a).wait_recv()
    total = m2[0]
    for j in range(1, chips):
        total = total + m2[j]
    m3[z] = total
    for d in range(1, np_):
        copy = remote(m3.at[z], m3.at[z], m3_s.at[d], m3_r.at[z], (z + d) % np_, a)
        copy.start()
        pending.append(copy)

    for d in range(chips - 1):
        remote(b2_out.at[d], b2_in.at[d], b2_s.at[d], b2_r.at[d], z, a).wait_recv()
        coupled = coupled + b2_in[d].astype(f32)
    mine = own_trial()
    values = own_gaps() * mine + 2.0 * coupled
    sigma[...] = values
    lane = lax.broadcasted_iota(jnp.int32, (vecs, 128), 1)
    sums = jnp.where(
        lane == 0,
        jnp.sum(values * values, axis=1, keepdims=True),
        jnp.where(lane == 1, jnp.sum(values * mine, axis=1, keepdims=True), 0.0),
    )
    n1[a] = jnp.transpose(sums)[:8]
    for d in range(1, na):
        copy = remote(n1.at[a], n1.at[a], n1_s.at[d], n1_r.at[a], z, (a + d) % na)
        copy.start()
        pending.append(copy)
    outs = [pltpu.make_async_copy(sigma, sigma_hbm, store.at[0])]
    outs[0].start()
    for d in range(1, na):
        j = (a + d) % na
        remote(n1.at[j], n1.at[j], n1_s.at[d], n1_r.at[j], z, j).wait_recv()
    sums = n1[0]
    for j in range(1, na):
        sums = sums + n1[j]
    n2[z] = sums
    for d in range(1, np_):
        copy = remote(n2.at[z], n2.at[z], n2_s.at[d], n2_r.at[z], (z + d) % np_, a)
        copy.start()
        pending.append(copy)

    for d in range(1, np_):
        j = (z + d) % np_
        remote(m3.at[j], m3.at[j], m3_s.at[d], m3_r.at[j], j, a).wait_recv()
    total = m3[0]
    for j in range(1, np_):
        total = total + m3[j]
    pairs = float(np_ * na * share)
    subspace = jnp.concatenate([total[:h, :vecs], total[:h, vecs:]], axis=0) / pairs
    sub[...] = subspace
    outs.append(pltpu.make_async_copy(sub, sub_hbm, store.at[1]))
    outs[1].start()
    squares = total[h:h + 1, :vecs]
    diagonal = jnp.sum(jnp.where(eye, subspace, 0.0), axis=0, keepdims=True)
    rayleigh = diagonal / (squares / pairs + epsilon)
    column = jnp.sum(jnp.where(eye, rayleigh, 0.0), axis=1, keepdims=True)
    res[...] = sigma[...] - own_trial() * column
    outs.append(pltpu.make_async_copy(res, res_hbm, store.at[2]))
    outs[2].start()

    for d in range(1, np_):
        j = (z + d) % np_
        remote(n2.at[j], n2.at[j], n2_s.at[d], n2_r.at[j], j, a).wait_recv()
    sums = n2[0]
    for j in range(1, np_):
        sums = sums + n2[j]
    residual_sq = sums[0:1] - 2.0 * rayleigh * sums[1:2] + rayleigh * rayleigh * squares
    norm[...] = jnp.sqrt(residual_sq / pairs + epsilon)
    outs.append(pltpu.make_async_copy(norm, norm_hbm, store.at[3]))
    outs[3].start()

    @pl.when(after > 0)
    def _():
        for c in range(chunks):
            prefix(c).wait_send()

    @pl.when(z > 0)
    def _():
        for c in range(chunks):
            suffix(c).wait_send()

    for copy in pending:
        copy.wait_send()
    for copy in outs:
        copy.wait()


def store_kernel(*refs):
    for i in range(4):
        refs[i + 4][...] = refs[i][...]


def solution(mesh):
    np_, na = mesh.shape["pair"], mesh.shape["aux"]
    chips = na // 2

    def local(integrals, energy_gaps, trial_vectors):
        rows, cols = integrals.shape
        vecs = trial_vectors.shape[1]
        width = WIDTH
        chunks, share = cols // width, rows // na
        anywhere = pl.BlockSpec(memory_space=pl.ANY)
        dma = pltpu.SemaphoreType.DMA
        message = (vecs // 2 + 8, 2 * vecs)
        results = pl.pallas_call(
            functools.partial(kernel, np_, na, chunks, width, share),
            out_shape=[
                jax.ShapeDtypeStruct((vecs, share), f32),
                jax.ShapeDtypeStruct((vecs, vecs), f32),
                jax.ShapeDtypeStruct((vecs, share), f32),
                jax.ShapeDtypeStruct((1, vecs), f32),
            ],
            in_specs=[anywhere] * 3,
            out_specs=[anywhere] * 4,
            scratch_shapes=[
                pltpu.VMEM((chunks, rows, width), bf16),
                pltpu.VMEM((rows // 128, 128), f32),
                pltpu.VMEM((vecs, rows), f32),
                pltpu.VMEM((vecs, rows), bf16),
                pltpu.VMEM((chunks, vecs, width), f32),
                pltpu.VMEM((na, vecs, share), f32),
                pltpu.VMEM((vecs, vecs), f32),
                pltpu.VMEM((vecs, vecs), f32),
                *[pltpu.VMEM((chunks, vecs, width), bf16)] * 4,
                *[pltpu.VMEM((chips, vecs, share), bf16)] * 4,
                pltpu.VMEM(message, f32),
                pltpu.VMEM(message, f32),
                pltpu.VMEM((chips,) + message, f32),
                pltpu.VMEM((np_,) + message, f32),
                pltpu.VMEM((na, 8, vecs), f32),
                pltpu.VMEM((np_, 8, vecs), f32),
                pltpu.VMEM((vecs, share), f32),
                pltpu.VMEM((vecs, vecs), f32),
                pltpu.VMEM((vecs, share), f32),
                pltpu.VMEM((1, vecs), f32),
                dma((chunks,)), dma((2,)),
                dma((chunks,)), dma((chunks,)), dma((chunks,)), dma((chunks,)),
                dma((chips,)), dma((chips,)), dma((chips,)), dma((chips,)),
                dma, dma, dma((chips,)), dma((chips,)),
                dma((np_,)), dma((np_,)), dma((na,)), dma((na,)), dma((np_,)), dma((np_,)),
                dma((4,)),
            ],
            compiler_params=pltpu.CompilerParams(
                collective_id=0, has_side_effects=True, vmem_limit_bytes=VMEM
            ),
            name="sigma_build",
        )(integrals, energy_gaps.reshape(rows // 128, 128), trial_vectors.T)
        sigma, subspace, residuals, norms = pl.pallas_call(
            store_kernel,
            out_shape=[jax.ShapeDtypeStruct(x.shape, x.dtype) for x in results],
            in_specs=[pl.BlockSpec(memory_space=pltpu.VMEM)] * 4,
            out_specs=[pl.BlockSpec(memory_space=pltpu.VMEM)] * 4,
            compiler_params=pltpu.CompilerParams(vmem_limit_bytes=VMEM),
            name="store",
        )(*results)
        return sigma.T, subspace, residuals.T, norms.reshape(vecs)

    return jax.shard_map(
        local,
        mesh=mesh,
        in_specs=(P("pair", "aux"), P("pair"), P("pair", None)),
        out_specs=(P(("pair", "aux"), None), P(), P(("pair", "aux"), None), P()),
        check_vma=False,
    )
```

profile of v0, /device:TPU:0, one launch (start us, length us, event | category | flops | bytes accessed | tf_op | source)
XLA Modules:
  0.0 37.8 jit_solution(18129522142780015815)
XLA Ops:
  0.6 35.5 %sigma_build.1 = (f32[64,384]{1,0:T(8,128)}, f32[64,64]{1,0:T(8,128)}, f32[64,384]{1,0:T(8,128)}, f32[1,64]{1,0:T(1,128)}) custom-call(bf16[3072,1536]{1,0:T(8,128)(2,1)} %ints_hbm.1, f32[24,128]{1,0:T(8,128)} %bitcast.6, f32[64,3072]{1,0:T(8,128)} %bitcast.5), custom_call_target="tpu_custom_call" | custom-call | tf_op jit(solution)/shard_map/sigma_build/pallas_call | solution.py:310
  36.1 1.7 %store.1 = (f32[64,384]{1,0:T(8,128)}, f32[64,64]{1,0:T(8,128)}, f32[64,384]{1,0:T(8,128)}, f32[1,64]{1,0:T(1,128)}) custom-call(f32[64,384]{1,0:T(8,128)} %get-tuple-element.12.refs_0_, f32[64,64]{1,0:T(8,128)} %get-tuple-element.13.refs_1_, f32[64,384]{1,0:T(8,128)} %get-tuple-element.14.refs_2_, f32[1,64]{1,0:T(1,128)} %get-tuple-element.15.refs_3_), custom_call_target="tpu_custom_call" | custom-call | tf_op jit(solution)/shard_map/store/pallas_call | solution.py:353
where the time goes:
time: 37.9 us; the launch traced here: 37.8 us
  Pallas kernels  37.1 us (98%)
  between operations  0.64 us (2%)
    pallas_call x1, Pallas kernels, local(): pl.pallas_call(functools.partial(kernel, np_, na, chunks, width, share),...  35.5 us
    pallas_call x1, Pallas kernels, local(): pl.pallas_call(store_kernel, out_shape=[jax.ShapeDtypeStruct(x.shape, x.d...  1.65 us

commit v1 on v0

--- a/solution.py
+++ b/solution.py
@@ -11,7 +11,7 @@
 MESH = pl.DeviceIdType.MESH
 f32, bf16 = jnp.float32, jnp.bfloat16
 WIDTH = 256
-VMEM = 67043328
+VMEM = 48 * 1024 * 1024
 LAG = 3
 NT = (((1,), (1,)), ((), ()))
 
@@ -23,14 +23,13 @@
 def kernel(
     np_, na, chunks, width, share,
     ints_hbm, gaps_hbm, trial_hbm,
-    sigma_hbm, sub_hbm, res_hbm, norm_hbm,
+    sigma, sub, res, norm,
     ints, gaps, trial, half, own, acc, mat, gram,
     pre_in, pre_out, suf_in, suf_out,
     b1_out, b1_in, b2_out, b2_in,
     m1_out, m1_in, m2, m3, n1, n2,
-    sigma, sub, res, norm,
     load, aload, pre_s, pre_r, suf_s, suf_r,
-    b1_s, b1_r, b2_s, b2_r, m1_s, m1_r, m2_s, m2_r, m3_s, m3_r, n1_s, n1_r, n2_s, n2_r, store,
+    b1_s, b1_r, b2_s, b2_r, m1_s, m1_r, m2_s, m2_r, m3_s, m3_r, n1_s, n1_r, n2_s, n2_r,
 ):
     z, a = lax.axis_index("pair"), lax.axis_index("aux")
     core, chip, chips = a % 2, a // 2, na // 2
@@ -230,8 +229,6 @@
         copy = remote(n1.at[a], n1.at[a], n1_s.at[d], n1_r.at[a], z, (a + d) % na)
         copy.start()
         pending.append(copy)
-    outs = [pltpu.make_async_copy(sigma, sigma_hbm, store.at[0])]
-    outs[0].start()
     for d in range(1, na):
         j = (a + d) % na
         remote(n1.at[j], n1.at[j], n1_s.at[d], n1_r.at[j], z, j).wait_recv()
@@ -253,15 +250,11 @@
     pairs = float(np_ * na * share)
     subspace = jnp.concatenate([total[:h, :vecs], total[:h, vecs:]], axis=0) / pairs
     sub[...] = subspace
-    outs.append(pltpu.make_async_copy(sub, sub_hbm, store.at[1]))
-    outs[1].start()
     squares = total[h:h + 1, :vecs]
     diagonal = jnp.sum(jnp.where(eye, subspace, 0.0), axis=0, keepdims=True)
     rayleigh = diagonal / (squares / pairs + epsilon)
     column = jnp.sum(jnp.where(eye, rayleigh, 0.0), axis=1, keepdims=True)
     res[...] = sigma[...] - own_trial() * column
-    outs.append(pltpu.make_async_copy(res, res_hbm, store.at[2]))
-    outs[2].start()
 
     for d in range(1, np_):
         j = (z + d) % np_
@@ -271,8 +264,6 @@
         sums = sums + n2[j]
     residual_sq = sums[0:1] - 2.0 * rayleigh * sums[1:2] + rayleigh * rayleigh * squares
     norm[...] = jnp.sqrt(residual_sq / pairs + epsilon)
-    outs.append(pltpu.make_async_copy(norm, norm_hbm, store.at[3]))
-    outs[3].start()
 
     @pl.when(after > 0)
     def _():
@@ -286,13 +277,15 @@
 
     for copy in pending:
         copy.wait_send()
-    for copy in outs:
+
+
+def store_kernel(*refs):
+    done = refs[8]
+    copies = [pltpu.make_async_copy(refs[i], refs[i + 4], done.at[i]) for i in range(4)]
+    for copy in copies:
+        copy.start()
+    for copy in copies:
         copy.wait()
-
-
-def store_kernel(*refs):
-    for i in range(4):
-        refs[i + 4][...] = refs[i][...]
 
 
 def solution(mesh):
@@ -315,8 +308,8 @@
                 jax.ShapeDtypeStruct((vecs, share), f32),
                 jax.ShapeDtypeStruct((1, vecs), f32),
             ],
-            in_specs=[anywhere] * 3,
-            out_specs=[anywhere] * 4,
+            in_specs=[pl.BlockSpec(memory_space=pltpu.HBM)] * 3,
+            out_specs=[pl.BlockSpec(memory_space=pltpu.VMEM)] * 4,
             scratch_shapes=[
                 pltpu.VMEM((chunks, rows, width), bf16),
                 pltpu.VMEM((rows // 128, 128), f32),
@@ -334,27 +327,23 @@
                 pltpu.VMEM((np_,) + message, f32),
                 pltpu.VMEM((na, 8, vecs), f32),
                 pltpu.VMEM((np_, 8, vecs), f32),
-                pltpu.VMEM((vecs, share), f32),
-                pltpu.VMEM((vecs, vecs), f32),
-                pltpu.VMEM((vecs, share), f32),
-                pltpu.VMEM((1, vecs), f32),
                 dma((chunks,)), dma((2,)),
                 dma((chunks,)), dma((chunks,)), dma((chunks,)), dma((chunks,)),
                 dma((chips,)), dma((chips,)), dma((chips,)), dma((chips,)),
                 dma, dma, dma((chips,)), dma((chips,)),
                 dma((np_,)), dma((np_,)), dma((na,)), dma((na,)), dma((np_,)), dma((np_,)),
-                dma((4,)),
             ],
             compiler_params=pltpu.CompilerParams(
                 collective_id=0, has_side_effects=True, vmem_limit_bytes=VMEM
             ),
             name="sigma_build",
-        )(integrals, energy_gaps.reshape(rows // 128, 128), trial_vectors.T)
+        )(*[pltpu.with_memory_space_constraint(x, pltpu.HBM) for x in (integrals, energy_gaps.reshape(rows // 128, 128), trial_vectors.T)])
         sigma, subspace, residuals, norms = pl.pallas_call(
             store_kernel,
             out_shape=[jax.ShapeDtypeStruct(x.shape, x.dtype) for x in results],
             in_specs=[pl.BlockSpec(memory_space=pltpu.VMEM)] * 4,
-            out_specs=[pl.BlockSpec(memory_space=pltpu.VMEM)] * 4,
+            out_specs=[anywhere] * 4,
+            scratch_shapes=[dma((4,))],
             compiler_params=pltpu.CompilerParams(vmem_limit_bytes=VMEM),
             name="store",
         )(*results)

time: 37.9 us -> 36.4 us (0.960)
  Pallas kernels: 37.1 us -> 35.6 us
    pallas_call x1, Pallas kernels: 1.65 us -> 0.72 us  [local(): pl.pallas_call(store_kernel, out_shape=[jax.ShapeDtypeStruct(x.shape, x.d...]
    pallas_call x1, Pallas kernels: 35.5 us -> 34.9 us  [local(): pl.pallas_call(functools.partial(kernel, np_, na, chunks, width, share),...]
where the time goes in v1:
time: 36.4 us; the launch traced here: 36.3 us
  Pallas kernels  35.6 us (98%)
  between operations  0.64 us (2%)
    pallas_call x1, Pallas kernels, local(): pl.pallas_call(functools.partial(kernel, np_, na, chunks, width, share),...  34.9 us

profile of v1, /device:TPU:0, one launch (start us, length us, event | category | flops | bytes accessed | tf_op | source)
XLA Modules:
  0.0 36.3 jit_solution(8468916229884810930)
XLA Ops:
  0.6 34.9 %sigma_build.1 = (f32[64,384]{1,0:T(8,128)S(1)}, f32[64,64]{1,0:T(8,128)S(1)}, f32[64,384]{1,0:T(8,128)S(1)}, f32[1,64]{1,0:T(1,128)S(1)}) custom-call(bf16[3072,1536]{1,0:T(8,128)(2,1)} %ints_hbm.1, f32[24,128]{1,0:T(8,128)} %bitcast.6, f32[64,3072]{1,0:T(8,128)} %bitcast.5), custom_call_target="tpu_custom_call" | custom-call | tf_op jit(solution)/shard_map/sigma_build/pallas_call | solution.py:303
  35.6 0.7 %store.1 = (f32[64,384]{1,0:T(8,128)}, f32[64,64]{1,0:T(8,128)}, f32[64,384]{1,0:T(8,128)}, f32[1,64]{1,0:T(1,128)}) custom-call(f32[64,384]{1,0:T(8,128)S(1)} %get-tuple-element.12.refs_0_, f32[64,64]{1,0:T(8,128)S(1)} %get-tuple-element.13.refs_1_, f32[64,384]{1,0:T(8,128)S(1)} %get-tuple-element.14.refs_2_, f32[1,64]{1,0:T(1,128)S(1)} %get-tuple-element.15.refs_3_), custom_call_target="tpu_custom_call" | custom-call | tf_op jit(solution)/shard_map/store/pallas_call | solution.py:341

commit v2 on v1

v2 whole, which is shorter than its diff:
```python
import functools

import jax
import jax.numpy as jnp
from jax import lax
from jax.experimental import pallas as pl
from jax.experimental.pallas import tpu as pltpu
from jax.sharding import PartitionSpec as P

epsilon = 1e-06
MESH = pl.DeviceIdType.MESH
f32, bf16 = jnp.float32, jnp.bfloat16
LANES = 128
VMEM = 48 * 1024 * 1024
LAG = 8
HOLD = 0
FIRST = 0
AHEAD = 3
NT = (((1,), (1,)), ((), ()))


def exact(a, b):
    return lax.dot_general(a, b, NT, precision=lax.Precision.HIGHEST, preferred_element_type=f32)


def kernel(
    np_, na, pieces, share,
    ints_hbm, gaps_hbm, trial_hbm,
    sigma, sub, res, norm,
    ints, gaps, trial, half, own, acc, mat,
    pre_in, pre_out, suf_in, suf_out,
    b1_out, b1_in, b2_out, b2_in,
    g_out, g_in, g3, m1_out, m1_in, m2, sums,
    load, aload, pre_s, pre_r, suf_s, suf_r,
    b1_s, b1_r, b2_s, b2_r, g_s, g_r, g3_s, g3_r, m1_s, m1_r, m2_s, m2_r, n_s, n_r,
):
    z, a = lax.axis_index("pair"), lax.axis_index("aux")
    core, chip, chips = a % 2, a // 2, na // 2
    vecs = trial.shape[0]
    h = vecs // 2
    chunks = pieces // 2
    devices = np_ * na
    me = z * na + a
    other = chip * 2 + 1 - core

    trial_load = pltpu.make_async_copy(trial_hbm, trial, aload.at[0])
    gaps_load = pltpu.make_async_copy(gaps_hbm, gaps, aload.at[1])
    trial_load.start()

    def piece_load(q):
        columns = pl.ds(pl.multiple_of(q * LANES, LANES), LANES)
        return pltpu.make_async_copy(ints_hbm.at[:, columns], ints.at[q], load.at[q])

    for q in range(2 * AHEAD):
        piece_load(q).start()
    gaps_load.start()

    barrier = pltpu.get_barrier_semaphore()
    after = np_ - 1 - z
    bits = [b for b in range(10) if 2 ** b < chips]

    def flip(b):
        return (chip + 2 ** b * (1 - 2 * (chip // 2 ** b % 2))) * 2 + core

    circle = [other] + [flip(b) for b in bits]

    def greet(pair, aux):
        pl.semaphore_signal(barrier, inc=1, device_id={"pair": pair, "aux": aux}, device_id_type=MESH)

    @pl.when(z > 0)
    def _():
        greet(z - 1, a)

    @pl.when(after > 0)
    def _():
        greet(z + 1, a)

    for aux in circle:
        greet(z, aux)

    def remote(src, dst, s, r, pair, aux):
        return pltpu.make_async_remote_copy(
            src_ref=src, dst_ref=dst, send_sem=s, recv_sem=r,
            device_id={"pair": pair, "aux": aux}, device_id_type=MESH,
        )

    def prefix(q):
        return remote(pre_out.at[q], pre_in.at[q], pre_s.at[q], pre_r.at[q], z + 1, a)

    def suffix(q):
        return remote(suf_out.at[q], suf_in.at[q], suf_s.at[q], suf_r.at[q], z - 1, a)

    first = pl.multiple_of(a * share, LANES)
    rows = share // LANES

    def own_trial():
        return trial[:, pl.ds(first, share)]

    def own_gaps():
        return jnp.concatenate([gaps[pl.ds(a * rows + q, 1), :] for q in range(rows)], axis=1)

    eye = lax.broadcasted_iota(jnp.int32, (vecs, vecs), 0) == lax.broadcasted_iota(jnp.int32, (vecs, vecs), 1)

    def as_row(column):
        return jnp.sum(jnp.where(eye, column, 0.0), axis=0, keepdims=True)

    acc[...] = jnp.zeros_like(acc)
    mat[...] = jnp.zeros_like(mat)
    trial_load.wait()
    half[...] = trial[...].astype(bf16)
    gaps_load.wait()
    mine = own_trial()
    gram = exact(mine, mine * own_gaps())
    squares = as_row(jnp.sum(mine * mine, axis=1, keepdims=True))
    g_out[0, 0:h] = jnp.concatenate([gram[:h], gram[h:]], axis=1)
    g_out[0, h:] = jnp.broadcast_to(jnp.concatenate([squares, squares], axis=1), (8, 2 * vecs))
    g_copies = [
        remote(g_out.at[i], g_in.at[i], g_s.at[i], g_r.at[i], z, aux) for i, aux in enumerate(circle)
    ]

    def g_next(i):
        g_copies[i - 1].wait_recv()
        g_out[i] = g_out[i - 1] + g_in[i - 1]
        g_copies[i].start()

    longest = jnp.maximum(z, after)
    inner = (z > 0) & (after > 0)
    hold = FIRST + core * HOLD

    def first_pass(c, carry):
        for k in range(2):
            piece_load(2 * c + k).wait()

        @pl.when(c + AHEAD < chunks)
        def _():
            for k in range(2):
                piece_load(2 * (c + AHEAD) + k).start()

        block = jnp.concatenate([ints[2 * c], ints[2 * c + 1]], axis=1)
        product = jnp.dot(half[...], block, preferred_element_type=f32)
        own[2 * c] = product[:, :LANES]
        own[2 * c + 1] = product[:, LANES:]

        @pl.when(c == FIRST)
        def _():
            pl.semaphore_wait(barrier, len(circle) + jnp.where(inner, 2, 1))
            g_copies[0].start()

        @pl.when(z == 0)
        def _():
            pre_out[2 * c] = own[2 * c].astype(bf16)
            pre_out[2 * c + 1] = own[2 * c + 1].astype(bf16)

        @pl.when(after == 0)
        def _():
            suf_out[2 * c] = own[2 * c].astype(bf16)
            suf_out[2 * c + 1] = own[2 * c + 1].astype(bf16)

        def send(b):
            @pl.when(z == 0)
            def _():
                prefix(2 * b).start()
                prefix(2 * b + 1).start()

            @pl.when(after == 0)
            def _():
                suffix(2 * b).start()
                suffix(2 * b + 1).start()

        @pl.when(c == hold)
        def _():
            lax.fori_loop(0, hold, lambda b, x: (send(b), x)[1], 0)

        @pl.when(c >= hold)
        def _():
            send(c)

        return carry

    lax.fori_loop(0, chunks, first_pass, 0)
    for i in range(1, min(2, len(circle))):
        g_next(i)
    base = jnp.where(inner, jnp.minimum(z, after), longest)

    def second_pass(q):
        total = own[q]
        aux = total.astype(bf16)
        low = (total - aux.astype(f32)).astype(bf16)
        return aux, lax.dot_general(
            jnp.concatenate([aux, low], axis=0), aux, NT, preferred_element_type=f32
        )

    def step(t, carry):
        p = t - LAG * (z - base)

        @pl.when((p >= 0) & (p < pieces) & inner)
        def _():
            prefix(p).wait_recv()
            pre_out[p] = (own[p] + pre_in[p].astype(f32)).astype(bf16)
            prefix(p).start()

        s = t - LAG * (after - base)

        @pl.when((s >= 0) & (s < pieces) & inner)
        def _():
            suffix(s).wait_recv()
            suf_out[s] = (own[s] + suf_in[s].astype(f32)).astype(bf16)
            suffix(s).start()

        q = t - LAG * (longest - base)

        @pl.when(q >= 0)
        def _():
            @pl.when(after == 0)
            def _():
                prefix(q).wait_recv()

            @pl.when(z == 0)
            def _():
                suffix(q).wait_recv()

            @pl.when(z > 0)
            def _():
                own[q] = own[q] + pre_in[q].astype(f32)

            @pl.when(after > 0)
            def _():
                own[q] = own[q] + suf_in[q].astype(f32)

            @pl.when(q < pieces - 1)
            def _():
                aux, square = second_pass(q)
                mat[...] += square
                for b in range(chips):
                    part = lax.dot_general(
                        aux, ints[q, pl.ds(b * 2 * share, 2 * share), :], NT, preferred_element_type=f32
                    )
                    acc[2 * b] += part[:, :share]
                    acc[2 * b + 1] += part[:, share:]

        @pl.when(t == jnp.where(inner, LAG - 1, 0))
        def _():
            for i in range(2, len(circle)):
                g_next(i)

        return carry

    lax.fori_loop(0, pieces + LAG * (longest - base), step, 0)

    pending = list(g_copies)
    g_copies[-1].wait_recv()
    aux, square = second_pass(pieces - 1)

    def chip_at(d):
        return (chip + jnp.where(chip % 2 == 1, d, chips - d)) % chips

    def last_part(i):
        return lax.dot_general(
            aux, ints[pieces - 1, pl.ds(pl.multiple_of(i * share, LANES), share), :], NT,
            preferred_element_type=f32,
        )

    b1 = []
    for d in range(1, chips + 1):
        i = 2 * chip_at(d) + 1 - core
        b1_out[d - 1] = (acc[i] + last_part(i)).astype(bf16)
        copy = remote(b1_out.at[d - 1], b1_in.at[d - 1], b1_s.at[d - 1], b1_r.at[d - 1], z, other)
        copy.start()
        b1.append(copy)
        pending.append(copy)
    for d in range(1, chips + 1):
        i = 2 * chip_at(d) + core
        acc[i] += last_part(i)
    square = mat[...] + square
    square = square[:vecs] + square[vecs:]
    m1_out[...] = jnp.concatenate([square[:h], square[h:]], axis=1)
    m1_copy = remote(m1_out, m1_in, m1_s, m1_r, z, other)
    m1_copy.start()
    pending.append(m1_copy)
    for d in range(1, chips):
        j = chip_at(d)
        b1[d - 1].wait_recv()
        b2_out[d - 1] = (acc[2 * j + core] + b1_in[d - 1].astype(f32)).astype(bf16)
        copy = remote(b2_out.at[d - 1], b2_in.at[d - 1], b2_s.at[d - 1], b2_r.at[d - 1], z, 2 * j + core)
        copy.start()
        pending.append(copy)
    b1[chips - 1].wait_recv()
    coupled = acc[a] + b1_in[chips - 1].astype(f32)

    g3[z] = g_out[len(circle) - 1] + g_in[len(circle) - 1]
    for d in range(1, np_):
        copy = remote(g3.at[z], g3.at[z], g3_s.at[d], g3_r.at[z], (z + d) % np_, a)
        copy.start()
        pending.append(copy)
    m1_copy.wait_recv()
    m2[chip] = m1_out[...] + m1_in[...]
    for d in range(1, chips):
        copy = remote(m2.at[chip], m2.at[chip], m2_s.at[d], m2_r.at[chip], z, ((chip + d) % chips) * 2 + core)
        copy.start()
        pending.append(copy)

    for d in range(1, chips):
        remote(b2_out.at[d - 1], b2_in.at[d - 1], b2_s.at[d - 1], b2_r.at[d - 1], z, a).wait_recv()
        coupled = coupled + b2_in[d - 1].astype(f32)
    mine = own_trial()
    values = own_gaps() * mine + 2.0 * coupled
    both = jnp.concatenate([values * values, values * mine], axis=0)
    folded = both[:, :LANES]
    for q in range(1, rows):
        folded = folded + both[:, q * LANES:(q + 1) * LANES]
    sums[me] = jnp.sum(jnp.transpose(folded), axis=0, keepdims=True)

    def tell(pair, aux):
        remote(sums.at[me], sums.at[me], n_s, n_r, pair, aux).start()

    def tell_plane(i, carry):
        pair = jnp.where(2 * z < np_, np_ - 1 - i, i)
        for d in range(1, na):
            tell(pair, (a + d) % na)

        @pl.when(pair != z)
        def _():
            tell(pair, a)

        return carry

    lax.fori_loop(0, np_, tell_plane, 0)
    sigma[...] = values

    for d in range(1, chips):
        j = (chip + d) % chips
        remote(m2.at[j], m2.at[j], m2_s.at[d], m2_r.at[j], z, a).wait_recv()
    square = m2[0]
    for j in range(1, chips):
        square = square + m2[j]
    for d in range(1, np_):
        j = (z + d) % np_
        remote(g3.at[j], g3.at[j], g3_s.at[d], g3_r.at[j], j, a).wait_recv()
    total = g3[0]
    for j in range(1, np_):
        total = total + g3[j]
    pairs = float(devices * share)
    packed = total[:h] + 2.0 * square
    subspace = jnp.concatenate([packed[:, :vecs], packed[:, vecs:]], axis=0) / pairs
    sub[...] = subspace
    squares = total[h:h + 1, :vecs]
    diagonal = jnp.sum(jnp.where(eye, subspace, 0.0), axis=0, keepdims=True)
    rayleigh = diagonal / (squares / pairs + epsilon)
    column = jnp.sum(jnp.where(eye, rayleigh, 0.0), axis=1, keepdims=True)
    res[...] = sigma[...] - own_trial() * column

    everyone = remote(sums.at[pl.ds(0, devices - 1)], sums.at[pl.ds(0, devices - 1)], n_s, n_r, z, other)
    everyone.wait_recv()
    both = jnp.sum(sums[...], axis=0)
    residual_sq = both[:, :vecs] - 2.0 * rayleigh * both[:, vecs:] + rayleigh * rayleigh * squares
    norm[...] = jnp.sqrt(residual_sq / pairs + epsilon)

    @pl.when(after > 0)
    def _():
        for q in range(pieces):
            prefix(q).wait_send()

    @pl.when(z > 0)
    def _():
        for q in range(pieces):
            suffix(q).wait_send()

    for copy in pending:
        copy.wait_send()
    everyone.wait_send()


def store_kernel(*refs):
    done = refs[8]
    copies = [pltpu.make_async_copy(refs[i], refs[i + 4], done.at[i]) for i in range(4)]
    for copy in copies:
        copy.start()
    for copy in copies:
        copy.wait()


def solution(mesh):
    np_, na = mesh.shape["pair"], mesh.shape["aux"]
    chips = na // 2

    def local(integrals, energy_gaps, trial_vectors):
        rows, cols = integrals.shape
        vecs = trial_vectors.shape[1]
        pieces, share = cols // LANES, rows // na
        anywhere = pl.BlockSpec(memory_space=pl.ANY)
        local_block = pl.BlockSpec(memory_space=pltpu.VMEM)
        dma = pltpu.SemaphoreType.DMA
        stages = 1 + (chips - 1).bit_length()
        message = (vecs // 2 + 8, 2 * vecs)
        matrix = (vecs // 2, 2 * vecs)
        inputs = (integrals, energy_gaps.reshape(rows // LANES, LANES), trial_vectors.T)
        results = pl.pallas_call(
            functools.partial(kernel, np_, na, pieces, share),
            out_shape=[
                jax.ShapeDtypeStruct((vecs, share), f32),
                jax.ShapeDtypeStruct((vecs, vecs), f32),
                jax.ShapeDtypeStruct((vecs, share), f32),
                jax.ShapeDtypeStruct((1, vecs), f32),
            ],
            in_specs=[anywhere] * 3,
            out_specs=[local_block] * 4,
            scratch_shapes=[
                pltpu.VMEM((pieces, rows, LANES), bf16),
                pltpu.VMEM((rows // LANES, LANES), f32),
                pltpu.VMEM((vecs, rows), f32),
                pltpu.VMEM((vecs, rows), bf16),
                pltpu.VMEM((pieces, vecs, LANES), f32),
                pltpu.VMEM((na, vecs, share), f32),
                pltpu.VMEM((2 * vecs, vecs), f32),
                *[pltpu.VMEM((pieces, vecs, LANES), bf16)] * 4,
                *[pltpu.VMEM((chips, vecs, share), bf16)] * 4,
                pltpu.VMEM((stages,) + message, f32),
                pltpu.VMEM((stages,) + message, f32),
                pltpu.VMEM((np_,) + message, f32),
                pltpu.VMEM(matrix, f32),
                pltpu.VMEM(matrix, f32),
                pltpu.VMEM((chips,) + matrix, f32),
                pltpu.VMEM((np_ * na, 1, 2 * vecs), f32),
                dma((pieces,)), dma((2,)),
                dma((pieces,)), dma((pieces,)), dma((pieces,)), dma((pieces,)),
                dma((chips,)), dma((chips,)), dma((chips,)), dma((chips,)),
                dma((stages,)), dma((stages,)), dma((np_,)), dma((np_,)),
                dma, dma, dma((chips,)), dma((chips,)), dma, dma,
            ],
            compiler_params=pltpu.CompilerParams(
                collective_id=0, has_side_effects=True, vmem_limit_bytes=VMEM
            ),
            name="sigma_build",
        )(*[pltpu.with_memory_space_constraint(x, pltpu.HBM) for x in inputs])
        sigma, subspace, residuals, norms = pl.pallas_call(
            store_kernel,
            out_shape=[jax.ShapeDtypeStruct(x.shape, x.dtype) for x in results],
            in_specs=[local_block] * 4,
            out_specs=[anywhere] * 4,
            scratch_shapes=[dma((4,))],
            compiler_params=pltpu.CompilerParams(vmem_limit_bytes=VMEM),
            name="store",
        )(*results)
        return sigma.T, subspace, residuals.T, norms.reshape(vecs)

    return jax.shard_map(
        local,
        mesh=mesh,
        in_specs=(P("pair", "aux"), P("pair"), P("pair", None)),
        out_specs=(P(("pair", "aux"), None), P(), P(("pair", "aux"), None), P()),
        check_vma=False,
    )
```

time: 36.4 us -> 32.5 us (0.89)
  Pallas kernels: 35.6 us -> 31.6 us
    pallas_call x1, Pallas kernels: 34.9 us -> 30.9 us  [local(): pl.pallas_call(functools.partial(kernel, np_, na, pieces, share), out_sha...]
where the time goes in v2:
time: 32.5 us; the launch traced here: 32.3 us
  Pallas kernels  31.6 us (97%)
  between operations  0.64 us (2%)
    pallas_call x1, Pallas kernels, local(): pl.pallas_call(functools.partial(kernel, np_, na, pieces, share), out_sha...  30.9 us
    pallas_call x1, Pallas kernels, local(): pl.pallas_call(store_kernel, out_shape=[jax.ShapeDtypeStruct(x.shape, x.d...  0.72 us

profile of v2, /device:TPU:0, one launch (start us, length us, event | category | flops | bytes accessed | tf_op | source)
XLA Modules:
  0.0 32.3 jit_solution(10947702344227967478)
XLA Ops:
  0.6 30.9 %sigma_build.1 = (f32[64,384]{1,0:T(8,128)S(1)}, f32[64,64]{1,0:T(8,128)S(1)}, f32[64,384]{1,0:T(8,128)S(1)}, f32[1,64]{1,0:T(1,128)S(1)}) custom-call(bf16[3072,1536]{1,0:T(8,128)(2,1)} %ints_hbm.1, f32[24,128]{1,0:T(8,128)} %bitcast.6, f32[64,3072]{1,0:T(8,128)} %bitcast.5), custom_call_target="tpu_custom_call" | custom-call | tf_op jit(solution)/shard_map/sigma_build/pallas_call | solution.py:397
  31.6 0.7 %store.1 = (f32[64,384]{1,0:T(8,128)}, f32[64,64]{1,0:T(8,128)}, f32[64,384]{1,0:T(8,128)}, f32[1,64]{1,0:T(1,128)}) custom-call(f32[64,384]{1,0:T(8,128)S(1)} %get-tuple-element.12.refs_0_, f32[64,64]{1,0:T(8,128)S(1)} %get-tuple-element.13.refs_1_, f32[64,384]{1,0:T(8,128)S(1)} %get-tuple-element.14.refs_2_, f32[1,64]{1,0:T(1,128)S(1)} %get-tuple-element.15.refs_3_), custom_call_target="tpu_custom_call" | custom-call | tf_op jit(solution)/shard_map/store/pallas_call | solution.py:435

commit v3 on v2

--- a/solution.py
+++ b/solution.py
@@ -12,9 +12,7 @@
 f32, bf16 = jnp.float32, jnp.bfloat16
 LANES = 128
 VMEM = 48 * 1024 * 1024
-LAG = 8
-HOLD = 0
-FIRST = 0
+WIDTH = 2 * LANES
 AHEAD = 3
 NT = (((1,), (1,)), ((), ()))
 
@@ -24,21 +22,20 @@
 
 
 def kernel(
-    np_, na, pieces, share,
+    np_, na, chunks, share,
     ints_hbm, gaps_hbm, trial_hbm,
     sigma, sub, res, norm,
     ints, gaps, trial, half, own, acc, mat,
-    pre_in, pre_out, suf_in, suf_out,
+    c_in, c_out, j_in,
     b1_out, b1_in, b2_out, b2_in,
     g_out, g_in, g3, m1_out, m1_in, m2, sums,
-    load, aload, pre_s, pre_r, suf_s, suf_r,
+    load, aload, c_s, c_r, j_s, j_r,
     b1_s, b1_r, b2_s, b2_r, g_s, g_r, g3_s, g3_r, m1_s, m1_r, m2_s, m2_r, n_s, n_r,
 ):
     z, a = lax.axis_index("pair"), lax.axis_index("aux")
     core, chip, chips = a % 2, a // 2, na // 2
     vecs = trial.shape[0]
     h = vecs // 2
-    chunks = pieces // 2
     devices = np_ * na
     me = z * na + a
     other = chip * 2 + 1 - core
@@ -47,12 +44,12 @@
     gaps_load = pltpu.make_async_copy(gaps_hbm, gaps, aload.at[1])
     trial_load.start()
 
-    def piece_load(q):
-        columns = pl.ds(pl.multiple_of(q * LANES, LANES), LANES)
-        return pltpu.make_async_copy(ints_hbm.at[:, columns], ints.at[q], load.at[q])
-
-    for q in range(2 * AHEAD):
-        piece_load(q).start()
+    def chunk_load(c):
+        columns = pl.ds(pl.multiple_of(c * WIDTH, WIDTH), WIDTH)
+        return pltpu.make_async_copy(ints_hbm.at[:, columns], ints.at[c], load.at[c])
+
+    for c in range(min(AHEAD, chunks)):
+        chunk_load(c).start()
     gaps_load.start()
 
     barrier = pltpu.get_barrier_semaphore()
@@ -77,6 +74,14 @@
 
     for aux in circle:
         greet(z, aux)
+
+    inner = (z > 0) & (after > 0)
+    near = jnp.where(z < after, 0, 1)
+    late = core == 0 if np_ == 4 else core < 0
+
+    @pl.when(jnp.logical_not(inner) & late)
+    def _():
+        greet(z + 2 - 4 * near, a)
 
     def remote(src, dst, s, r, pair, aux):
         return pltpu.make_async_remote_copy(
@@ -84,12 +89,13 @@
             device_id={"pair": pair, "aux": aux}, device_id_type=MESH,
         )
 
-    def prefix(q):
-        return remote(pre_out.at[q], pre_in.at[q], pre_s.at[q], pre_r.at[q], z + 1, a)
-
-    def suffix(q):
-        return remote(suf_out.at[q], suf_in.at[q], suf_s.at[q], suf_r.at[q], z - 1, a)
-
+    def chain(k, c):
+        return remote(c_out.at[k, c], c_in.at[k, c], c_s.at[k, c], c_r.at[k, c], z + 1 - 2 * k, a)
+
+    def jump(c):
+        return remote(c_out.at[near, c], j_in.at[c], j_s.at[c], j_r.at[c], z + 2 - 4 * near, a)
+
+    cut = jnp.where(late, 0, chunks)
     first = pl.multiple_of(a * share, LANES)
     rows = share // LANES
 
@@ -123,140 +129,114 @@
         g_out[i] = g_out[i - 1] + g_in[i - 1]
         g_copies[i].start()
 
-    longest = jnp.maximum(z, after)
-    inner = (z > 0) & (after > 0)
-    hold = FIRST + core * HOLD
-
     def first_pass(c, carry):
-        for k in range(2):
-            piece_load(2 * c + k).wait()
+        chunk_load(c).wait()
 
         @pl.when(c + AHEAD < chunks)
         def _():
-            for k in range(2):
-                piece_load(2 * (c + AHEAD) + k).start()
-
-        block = jnp.concatenate([ints[2 * c], ints[2 * c + 1]], axis=1)
-        product = jnp.dot(half[...], block, preferred_element_type=f32)
-        own[2 * c] = product[:, :LANES]
-        own[2 * c + 1] = product[:, LANES:]
-
-        @pl.when(c == FIRST)
-        def _():
-            pl.semaphore_wait(barrier, len(circle) + jnp.where(inner, 2, 1))
+            chunk_load(c + AHEAD).start()
+
+        product = jnp.dot(half[...], ints[c], preferred_element_type=f32)
+        own[c] = product
+
+        @pl.when(c == 0)
+        def _():
+            pl.semaphore_wait(barrier, len(circle) + jnp.where(inner, jnp.where(late, 3, 2), 1))
             g_copies[0].start()
 
-        @pl.when(z == 0)
-        def _():
-            pre_out[2 * c] = own[2 * c].astype(bf16)
-            pre_out[2 * c + 1] = own[2 * c + 1].astype(bf16)
-
-        @pl.when(after == 0)
-        def _():
-            suf_out[2 * c] = own[2 * c].astype(bf16)
-            suf_out[2 * c + 1] = own[2 * c + 1].astype(bf16)
-
-        def send(b):
-            @pl.when(z == 0)
-            def _():
-                prefix(2 * b).start()
-                prefix(2 * b + 1).start()
-
-            @pl.when(after == 0)
-            def _():
-                suffix(2 * b).start()
-                suffix(2 * b + 1).start()
-
-        @pl.when(c == hold)
-        def _():
-            lax.fori_loop(0, hold, lambda b, x: (send(b), x)[1], 0)
-
-        @pl.when(c >= hold)
-        def _():
-            send(c)
+        @pl.when(jnp.logical_not(inner))
+        def _():
+            c_out[near, c] = product.astype(bf16)
+            chain(near, c).start()
+
+        @pl.when(inner & (c >= cut))
+        def _():
+            c_out[1 - near, c] = product.astype(bf16)
+            chain(1 - near, c).start()
 
         return carry
 
     lax.fori_loop(0, chunks, first_pass, 0)
     for i in range(1, min(2, len(circle))):
         g_next(i)
-    base = jnp.where(inner, jnp.minimum(z, after), longest)
-
-    def second_pass(q):
-        total = own[q]
+
+    def forward(k, c):
+        chain(k, c).wait_recv()
+        c_out[k, c] = (own[c] + c_in[k, c].astype(f32)).astype(bf16)
+        chain(k, c).start()
+
+    def near_step(c, carry):
+        forward(near, c)
+
+        @pl.when(c >= cut)
+        def _():
+            jump(c).start()
+
+        return carry
+
+    def far_step(c, carry):
+        forward(1 - near, c)
+        return carry
+
+    @pl.when(inner)
+    def _():
+        lax.fori_loop(0, chunks, near_step, 0)
+
+    for i in range(2, len(circle)):
+        g_next(i)
+
+    @pl.when(inner)
+    def _():
+        lax.fori_loop(0, cut, far_step, 0)
+
+    def total_of(c):
+        @pl.when(jnp.logical_not(inner) | (c >= cut))
+        def _():
+            chain(1 - near, c).wait_recv()
+
+        own[c] = own[c] + c_in[1 - near, c].astype(f32)
+
+        @pl.when(inner)
+        def _():
+            own[c] = own[c] + c_in[near, c].astype(f32)
+
+        @pl.when(jnp.logical_not(inner) & (c >= cut))
+        def _():
+            jump(c).wait_recv()
+            own[c] = own[c] + j_in[c].astype(f32)
+
+        total = own[c]
         aux = total.astype(bf16)
         low = (total - aux.astype(f32)).astype(bf16)
         return aux, lax.dot_general(
             jnp.concatenate([aux, low], axis=0), aux, NT, preferred_element_type=f32
         )
 
-    def step(t, carry):
-        p = t - LAG * (z - base)
-
-        @pl.when((p >= 0) & (p < pieces) & inner)
-        def _():
-            prefix(p).wait_recv()
-            pre_out[p] = (own[p] + pre_in[p].astype(f32)).astype(bf16)
-            prefix(p).start()
-
-        s = t - LAG * (after - base)
-
-        @pl.when((s >= 0) & (s < pieces) & inner)
-        def _():
-            suffix(s).wait_recv()
-            suf_out[s] = (own[s] + suf_in[s].astype(f32)).astype(bf16)
-            suffix(s).start()
-
-        q = t - LAG * (longest - base)
-
-        @pl.when(q >= 0)
-        def _():
-            @pl.when(after == 0)
-            def _():
-                prefix(q).wait_recv()
-
-            @pl.when(z == 0)
-            def _():
-                suffix(q).wait_recv()
-
-            @pl.when(z > 0)
-            def _():
-                own[q] = own[q] + pre_in[q].astype(f32)
-
-            @pl.when(after > 0)
-            def _():
-                own[q] = own[q] + suf_in[q].astype(f32)
-
-            @pl.when(q < pieces - 1)
-            def _():
-                aux, square = second_pass(q)
-                mat[...] += square
-                for b in range(chips):
-                    part = lax.dot_general(
-                        aux, ints[q, pl.ds(b * 2 * share, 2 * share), :], NT, preferred_element_type=f32
-                    )
-                    acc[2 * b] += part[:, :share]
-                    acc[2 * b + 1] += part[:, share:]
-
-        @pl.when(t == jnp.where(inner, LAG - 1, 0))
-        def _():
-            for i in range(2, len(circle)):
-                g_next(i)
-
+    def second_pass(i, carry):
+        c = (i + cut) % chunks
+        aux, square = total_of(c)
+        mat[...] += square
+        for b in range(chips):
+            part = lax.dot_general(
+                aux, ints[c, pl.ds(b * 2 * share, 2 * share), :], NT, preferred_element_type=f32
+            )
+            acc[2 * b] += part[:, :share]
+            acc[2 * b + 1] += part[:, share:]
         return carry
 
-    lax.fori_loop(0, pieces + LAG * (longest - base), step, 0)
+    lax.fori_loop(0, chunks - 1, second_pass, 0)
 
     pending = list(g_copies)
     g_copies[-1].wait_recv()
-    aux, square = second_pass(pieces - 1)
+    last = (chunks - 1 + cut) % chunks
+    aux, square = total_of(last)
 
     def chip_at(d):
         return (chip + jnp.where(chip % 2 == 1, d, chips - d)) % chips
 
     def last_part(i):
         return lax.dot_general(
-            aux, ints[pieces - 1, pl.ds(pl.multiple_of(i * share, LANES), share), :], NT,
+            aux, ints[last, pl.ds(pl.multiple_of(i * share, LANES), share), :], NT,
             preferred_element_type=f32,
         )
 
@@ -357,13 +337,17 @@
 
     @pl.when(after > 0)
     def _():
-        for q in range(pieces):
-            prefix(q).wait_send()
+        for c in range(chunks):
+            chain(0, c).wait_send()
 
     @pl.when(z > 0)
     def _():
-        for q in range(pieces):
-            suffix(q).wait_send()
+        for c in range(chunks):
+            chain(1, c).wait_send()
+
+    @pl.when(inner)
+    def _():
+        lax.fori_loop(cut, chunks, lambda c, x: (jump(c).wait_send(), x)[1], 0)
 
     for copy in pending:
         copy.wait_send()
@@ -386,7 +370,7 @@
     def local(integrals, energy_gaps, trial_vectors):
         rows, cols = integrals.shape
         vecs = trial_vectors.shape[1]
-        pieces, share = cols // LANES, rows // na
+        chunks, share = cols // WIDTH, rows // na
         anywhere = pl.BlockSpec(memory_space=pl.ANY)
         local_block = pl.BlockSpec(memory_space=pltpu.VMEM)
         dma = pltpu.SemaphoreType.DMA
@@ -395,7 +379,7 @@
         matrix = (vecs // 2, 2 * vecs)
         inputs = (integrals, energy_gaps.reshape(rows // LANES, LANES), trial_vectors.T)
         results = pl.pallas_call(
-            functools.partial(kernel, np_, na, pieces, share),
+            functools.partial(kernel, np_, na, chunks, share),
             out_shape=[
                 jax.ShapeDtypeStruct((vecs, share), f32),
                 jax.ShapeDtypeStruct((vecs, vecs), f32),
@@ -405,14 +389,15 @@
             in_specs=[anywhere] * 3,
             out_specs=[local_block] * 4,
             scratch_shapes=[
-                pltpu.VMEM((pieces, rows, LANES), bf16),
+                pltpu.VMEM((chunks, rows, WIDTH), bf16),
                 pltpu.VMEM((rows // LANES, LANES), f32),
                 pltpu.VMEM((vecs, rows), f32),
                 pltpu.VMEM((vecs, rows), bf16),
-                pltpu.VMEM((pieces, vecs, LANES), f32),
+                pltpu.VMEM((chunks, vecs, WIDTH), f32),
                 pltpu.VMEM((na, vecs, share), f32),
                 pltpu.VMEM((2 * vecs, vecs), f32),
-                *[pltpu.VMEM((pieces, vecs, LANES), bf16)] * 4,
+                *[pltpu.VMEM((2, chunks, vecs, WIDTH), bf16)] * 2,
+                pltpu.VMEM((chunks, vecs, WIDTH), bf16),
                 *[pltpu.VMEM((chips, vecs, share), bf16)] * 4,
                 pltpu.VMEM((stages,) + message, f32),
                 pltpu.VMEM((stages,) + message, f32),
@@ -421,8 +406,8 @@
                 pltpu.VMEM(matrix, f32),
                 pltpu.VMEM((chips,) + matrix, f32),
                 pltpu.VMEM((np_ * na, 1, 2 * vecs), f32),
-                dma((pieces,)), dma((2,)),
-                dma((pieces,)), dma((pieces,)), dma((pieces,)), dma((pieces,)),
+                dma((chunks,)), dma((2,)),
+                dma((2, chunks)), dma((2, chunks)), dma((chunks,)), dma((chunks,)),
                 dma((chips,)), dma((chips,)), dma((chips,)), dma((chips,)),
                 dma((stages,)), dma((stages,)), dma((np_,)), dma((np_,)),
                 dma, dma, dma((chips,)), dma((chips,)), dma, dma,

time: 32.5 us -> 30.6 us (0.942)
  Pallas kernels: 31.6 us -> 29.7 us
    pallas_call x1, Pallas kernels: 30.9 us -> 29 us  [local(): pl.pallas_call(functools.partial(kernel, np_, na, chunks, share), out_sha...]
where the time goes in v3:
time: 30.6 us; the launch traced here: 30.4 us
  Pallas kernels  29.7 us (97%)
  between operations  0.64 us (2%)
    pallas_call x1, Pallas kernels, local(): pl.pallas_call(functools.partial(kernel, np_, na, chunks, share), out_sha...  29 us
    pallas_call x1, Pallas kernels, local(): pl.pallas_call(store_kernel, out_shape=[jax.ShapeDtypeStruct(x.shape, x.d...  0.72 us

profile of v3, /device:TPU:0, one launch (start us, length us, event | category | flops | bytes accessed | tf_op | source)
XLA Modules:
  0.0 30.4 jit_solution(13575983428080313006)
XLA Ops:
  0.6 29.0 %sigma_build.1 = (f32[64,384]{1,0:T(8,128)S(1)}, f32[64,64]{1,0:T(8,128)S(1)}, f32[64,384]{1,0:T(8,128)S(1)}, f32[1,64]{1,0:T(1,128)S(1)}) custom-call(bf16[3072,1536]{1,0:T(8,128)(2,1)} %ints_hbm.1, f32[24,128]{1,0:T(8,128)} %bitcast.6, f32[64,3072]{1,0:T(8,128)} %bitcast.5), custom_call_target="tpu_custom_call" | custom-call | tf_op jit(solution)/shard_map/sigma_build/pallas_call | solution.py:381
  29.7 0.7 %store.1 = (f32[64,384]{1,0:T(8,128)}, f32[64,64]{1,0:T(8,128)}, f32[64,384]{1,0:T(8,128)}, f32[1,64]{1,0:T(1,128)}) custom-call(f32[64,384]{1,0:T(8,128)S(1)} %get-tuple-element.12.refs_0_, f32[64,64]{1,0:T(8,128)S(1)} %get-tuple-element.13.refs_1_, f32[64,384]{1,0:T(8,128)S(1)} %get-tuple-element.14.refs_2_, f32[1,64]{1,0:T(1,128)S(1)} %get-tuple-element.15.refs_3_), custom_call_target="tpu_custom_call" | custom-call | tf_op jit(solution)/shard_map/store/pallas_call | solution.py:420
